TPU v7x, 32 devices: a whole 2x2x4 slice. The times are simulated.
32 devices in a mesh: rows: 4 (over z), tp: 4 (over y, x), unit: 2 (over core).
Axes of the slice: x: 2, y: 2, z: 4, core: 2. Of those that a mesh axis runs over, the one named last changes fastest.
Arguments:
- train_query: bfloat16 [4096, 2048], P(('unit', 'rows'), 'tp'), parts along dimension 0, may hold values from -0.125 to 0.125
- low_query: bfloat16 [4096, 64], P(('unit', 'rows')), parts along dimension 0, may hold values from -0.125 to 0.125
- high_query: bfloat16 [128, 2048], P('unit', 'tp'), parts along dimension 0, may hold values from -0.75 to 0.75
- train_key: bfloat16 [4096, 512], P(('unit', 'rows'), 'tp'), parts along dimension 0, may hold values from -0.125 to 0.125
- low_key: bfloat16 [4096, 64], P(('unit', 'rows')), parts along dimension 0, may hold values from -0.125 to 0.125
- high_key: bfloat16 [128, 512], P('unit', 'tp'), parts along dimension 0, may hold values from -0.75 to 0.75
- train_value: bfloat16 [4096, 512], P(('unit', 'rows'), 'tp'), parts along dimension 0, may hold values from -0.125 to 0.125
- low_value: bfloat16 [4096, 64], P(('unit', 'rows')), parts along dimension 0, may hold values from -0.125 to 0.125
- high_value: bfloat16 [128, 512], P('unit', 'tp'), parts along dimension 0, may hold values from -0.75 to 0.75
- norm_train: float32 [4096], P(('unit', 'rows', 'tp')), parts along dimension 0, may hold values from 0.25 to 1.75
- norm_step: float32 [4096], P(('unit', 'rows', 'tp')), parts along dimension 0, may hold values from -0.3 to 0.3
Outputs:
- final_query: bfloat16 [4096, 2048], P(('unit', 'tp')), parts along dimension 0
- final_key: bfloat16 [1024, 2048], P(('unit', 'tp')), parts along dimension 0
- final_value: bfloat16 [1024, 2048], P(('unit', 'tp')), parts along dimension 0
- serve_norm: bfloat16 [4096], P('unit'), parts along dimension 0
There are 2 independent parts, one for each index of `unit`. A program takes and returns all parts, laid end to end along the dimension named above; each array names one. Nothing has to cross between parts.
All inputs are finite; a program needn't handle non-finite values.
Results may differ from a plain program's by a relative error of at most 0.001.
Values may be sent and summed in bfloat16 or wider, within the bound.
A program may use at most 64 MiB of HBM per device.

v0:
```python
import jax
import jax.numpy as jnp
from jax import lax
from jax.sharding import PartitionSpec as P

mix_rate = 0.5


def shards(
    train_query,
    low_query,
    high_query,
    train_key,
    low_key,
    high_key,
    train_value,
    low_value,
    high_value,
    norm_train,
    norm_step,
):
    result_query = train_query.astype(jnp.float32) + mix_rate * jnp.dot(
        low_query, high_query, preferred_element_type=jnp.float32
    )
    result_key = train_key.astype(jnp.float32) + mix_rate * jnp.dot(
        low_key, high_key, preferred_element_type=jnp.float32
    )
    result_value = train_value.astype(jnp.float32) + mix_rate * jnp.dot(
        low_value, high_value, preferred_element_type=jnp.float32
    )
    narrow_query, narrow_key, narrow_value = (
        result_query.astype(jnp.bfloat16),
        result_key.astype(jnp.bfloat16),
        result_value.astype(jnp.bfloat16),
    )
    final_query, final_key, final_value = (
        lax.all_gather(narrow_query, "rows", axis=0, tiled=True),
        lax.all_gather(narrow_key, "rows", axis=0, tiled=True),
        lax.all_gather(narrow_value, "rows", axis=0, tiled=True),
    )
    final_query, final_key, final_value = (final_query.T, final_key.T, final_value.T)
    serve_norm = lax.all_gather(
        (norm_train + norm_step).astype(jnp.bfloat16), ("rows", "tp"), axis=0, tiled=True
    )
    return (final_query, final_key, final_value, serve_norm)


def solution(mesh):
    in_specs = (
        P(("unit", "rows"), "tp"),
        P(("unit", "rows"), None),
        P("unit", "tp"),
        P(("unit", "rows"), "tp"),
        P(("unit", "rows"), None),
        P("unit", "tp"),
        P(("unit", "rows"), "tp"),
        P(("unit", "rows"), None),
        P("unit", "tp"),
        P(("unit", "rows", "tp")),
        P(("unit", "rows", "tp")),
    )
    out_specs = (
        P(("unit", "tp"), None),
        P(("unit", "tp"), None),
        P(("unit", "tp"), None),
        P("unit"),
    )
    return jax.shard_map(shards, mesh=mesh, in_specs=in_specs, out_specs=out_specs, check_vma=False)
```

profile of v0, /device:TPU:0, one launch (start us, length us, event | category | flops | bytes accessed | tf_op | source)
XLA Modules:
  0.0 108.7 jit_solution(17795586656834404858)
XLA Ops:
  7.2 0.0 copy-start
  7.2 0.0 copy-start.1
  7.2 0.0 copy-start.2
  7.2 0.0 copy-start.3
  7.2 0.0 all-gather.3.cloned.1.call-start
  7.3 0.8 copy-done
  8.0 2.2 %fusion.1 = bf16[512,512]{1,0:T(8,128)(2,1)} fusion(bf16[512,64]{0,1:T(8,128)(2,1)S(1)} %copy-done, bf16[64,512]{1,0:T(8,128)(2,1)} %param.13, bf16[512,512]{1,0:T(8,128)(2,1)} %param.11), kind=kOutput, calls=%fused_computation.2 | convolution fusion | flops 34603008 | bytes 1179648 | tf_op jit(solution)/shard_map/dot_general | solution.py:22
  10.2 0.0 all-gather.3.cloned.1.call-update
  10.2 0.0 copy-start.4
  10.2 0.0 copy-start.5
  10.3 1.2 %fusion.4 = bf16[512,128]{1,0:T(8,128)(2,1)S(1)} fusion(bf16[512,64]{0,1:T(8,128)(2,1)} %param.15, bf16[64,128]{1,0:T(8,128)(2,1)} %param.16, bf16[512,128]{1,0:T(8,128)(2,1)} %param.14), kind=kOutput, calls=%fused_computation.7 | convolution fusion | flops 8650752 | bytes 344064 | tf_op jit(solution)/shard_map/dot_general | solution.py:25
  11.4 22.0 %all_gather.13 = bf16[2048,128]{1,0:T(8,128)(2,1)S(1)} all-gather(bf16[512,128]{1,0:T(8,128)(2,1)S(1)} %fusion.4), channel_id=1, replica_groups=mesh['rows'=4,'tp'=4,'unit'=2] {'rows'}, dimensions={0}, use_global_device_ids=true | all-gather | bytes 655360 | tf_op jit(solution)/shard_map/all_gather | solution.py:38
  33.4 1.0 copy.22
  34.4 0.0 copy-done.1
  34.5 0.0 copy-done.2
  34.5 0.0 copy-done.3
  34.5 0.2 fusion.5
  34.7 21.7 %all_gather.14 = bf16[2048,128]{1,0:T(8,128)(2,1)S(1)} all-gather(bf16[512,128]{1,0:T(8,128)(2,1)S(1)} %fusion.5), channel_id=1, replica_groups=mesh['rows'=4,'tp'=4,'unit'=2] {'rows'}, dimensions={0}, use_global_device_ids=true | all-gather | bytes 655360 | tf_op jit(solution)/shard_map/all_gather | solution.py:39
  56.4 1.0 copy.23
  57.4 0.0 copy-done.4
  57.4 0.0 copy-done.5
  57.4 39.9 %all-gather = bf16[16,1,128]{2,1,0:T(2,128)(2,1)S(1)} all-gather(bf16[1,1,128]{2,1,0:T(2,128)(2,1)S(1)} %convert_bitcast_fusion), channel_id=1, replica_groups=mesh['rows'=4,'tp'=4,'unit'=2] {'rows','tp'}, dimensions={0}, use_global_device_ids=true | all-gather | bytes 4352 | tf_op jit(solution)/shard_map/all_gather | solution.py:42
  97.3 0.6 reduce
  98.0 3.9 %copy.21 = bf16[512,2048]{1,0:T(8,128)(2,1)} copy(bf16[512,2048]{0,1:T(8,128)(2,1)} %bitcast.14) | data formatting | bytes 4194304
  (2 shorter events, 0.0 us)
Async XLA Ops:
  7.2 0.8 copy-start
  7.2 27.3 %copy-start.1 = (bf16[512,128]{1,0:T(8,128)(2,1)S(1)}, bf16[512,128]{1,0:T(8,128)(2,1)}, u32[]{:S(2)}) copy-start(bf16[512,128]{1,0:T(8,128)(2,1)} %param.17) | copy-start | bytes 393220
  7.2 27.3 %copy-start.2 = (bf16[512,64]{0,1:T(8,128)(2,1)S(1)}, bf16[512,64]{0,1:T(8,128)(2,1)}, u32[]{:S(2)}) copy-start(bf16[512,64]{0,1:T(8,128)(2,1)} %param.18) | copy-start | bytes 196612
  7.2 27.3 %copy-start.3 = (bf16[64,128]{1,0:T(8,128)(2,1)S(1)}, bf16[64,128]{1,0:T(8,128)(2,1)}, u32[]{:S(2)}) copy-start(bf16[64,128]{1,0:T(8,128)(2,1)} %param.19) | copy-start | bytes 49156
  7.2 90.7 %all-gather.3.cloned.1.call-start = ((), (), s32[]{:S(2)}) async-start(), calls=%async_computation | async-start | bytes 2621440 | tf_op jit(solution)/shard_map/all_gather | solution.py:37
  10.2 47.2 %copy-start.4 = (f32[128]{0:T(128)S(1)}, f32[128]{0:T(128)}, u32[]{:S(2)}) copy-start(f32[128]{0:T(128)} %param.20) | copy-start | bytes 1540
  10.2 47.2 %copy-start.5 = (f32[128]{0:T(128)S(1)}, f32[128]{0:T(128)}, u32[]{:S(2)}) copy-start(f32[128]{0:T(128)} %param.21) | copy-start | bytes 1540
Sparse Core Ops, SparseCore 0:
  10.3 60.1 all-gather.2
where the time goes:
time: 109 us
  blocking collectives  83.6 us (77%)
  between operations  14.1 us (13%)
  local copies, waits for them, and re-layouts  6.71 us (6%)
  matrix products  3.58 us (3%)
    all_gather x1, blocking collectives, shards(): lax.all_gather((norm_train + norm_step).astype(jnp.bfloat16), ('rows', 't...  39.9 us
    all_gather x1, blocking collectives, shards(): lax.all_gather(narrow_key, 'rows', axis=0, tiled=True)  22 us
    all_gather x1, blocking collectives, shards(): lax.all_gather(narrow_value, 'rows', axis=0, tiled=True)  21.7 us
    unnamed x15, local copies, waits for them, and re-layouts  6.71 us
    dot_general x1, matrix products, shards(): jnp.dot(low_query, high_query, preferred_element_type=jnp.float32)  2.19 us
  transfers between devices with their start and end apart: 1, of which 0 were waited for; matrix products, arithmetic and copies ran while one was open for 4% of the time, Pallas kernels for 0%

commit v1 on v0

--- a/solution.py
+++ b/solution.py
@@ -39,9 +39,11 @@
         lax.all_gather(narrow_value, "rows", axis=0, tiled=True),
     )
     final_query, final_key, final_value = (final_query.T, final_key.T, final_value.T)
-    serve_norm = lax.all_gather(
-        (norm_train + norm_step).astype(jnp.bfloat16), ("rows", "tp"), axis=0, tiled=True
-    )
+    part = (norm_train + norm_step).astype(jnp.bfloat16)
+    n_dev = lax.axis_size(("rows", "tp"))
+    tiles = jnp.stack([part for _ in range(n_dev)])
+    tiles = lax.all_to_all(tiles, ("rows", "tp"), split_axis=0, concat_axis=0)
+    serve_norm = jnp.concatenate(tiles, axis=0)
     return (final_query, final_key, final_value, serve_norm)
 
 

time: 109 us -> 86.7 us (0.80)
  blocking collectives: 83.6 us -> 45.5 us
  starting transfers between devices: 0.04 us -> 8.38 us
  waiting for transfers between devices: 0.02 us -> 6.28 us
    all_gather x1 -> x0, blocking collectives: 39.9 us -> none  [shards(): lax.all_gather((norm_train + norm_step).astype(jnp.bfloat16), ('rows', 't...]
    all_to_all x0 -> x1, starting transfers between devices: none -> 8.34 us  [shards(): tiles = lax.all_to_all(tiles, ('rows', 'tp'), split_axis=0, concat_axis=0)]
    all_gather x1, waiting for transfers between devices: 0.01 us -> 6.26 us  [shards(): lax.all_gather(narrow_query, 'rows', axis=0, tiled=True)]
    all_gather x1, blocking collectives: 22 us -> 23.2 us  [shards(): lax.all_gather(narrow_key, 'rows', axis=0, tiled=True)]
    unnamed x15 -> x11, local copies, waits for them, and re-layouts: 6.71 us -> 6.7 us
  transfers between devices with their start and end apart: 1 -> 2, of which waited for: 0 -> 1; matrix products, arithmetic and copies ran while one was open for 4% -> 6% of each run, Pallas kernels for 0% -> 0%
where the time goes in v1:
time: 86.7 us; the launch traced here: 86.4 us
  blocking collectives  45.5 us (52%)
  between operations  14.1 us (16%)
  starting transfers between devices  8.38 us (10%)
  local copies, waits for them, and re-layouts  7.29 us (8%)
  waiting for transfers between devices  6.28 us (7%)
  matrix products  3.6 us (4%)
  other arithmetic  1.3 us (1%)
    all_gather x1, blocking collectives, shards(): lax.all_gather(narrow_key, 'rows', axis=0, tiled=True)  23.2 us
    all_gather x1, blocking collectives, shards(): lax.all_gather(narrow_value, 'rows', axis=0, tiled=True)  22.3 us
    all_to_all x1, starting transfers between devices, shards(): tiles = lax.all_to_all(tiles, ('rows', 'tp'), split_axis=0, concat_axis=0)  8.34 us
    unnamed x11, local copies, waits for them, and re-layouts  6.7 us
    all_gather x1, waiting for transfers between devices, shards(): lax.all_gather(narrow_query, 'rows', axis=0, tiled=True)  6.26 us
    dot_general x1, matrix products, shards(): jnp.dot(low_query, high_query, preferred_element_type=jnp.float32)  2.19 us
  transfers between devices with their start and end apart: 2, of which 1 were waited for; matrix products, arithmetic and copies ran while one was open for 6% of the time, Pallas kernels for 0%

profile of v1, /device:TPU:0, one launch (start us, length us, event | category | flops | bytes accessed | tf_op | source)
XLA Modules:
  0.0 86.4 jit_solution(15022940838301561241)
XLA Ops:
  7.2 0.0 copy-start
  7.2 0.0 copy-start.1
  7.2 0.0 copy-start.2
  7.2 0.0 copy-start.3
  7.2 0.0 all-gather.2.cloned.1.call-start
  7.3 0.8 copy-done
  8.0 2.2 %fusion.1 = bf16[512,512]{1,0:T(8,128)(2,1)} fusion(bf16[512,64]{0,1:T(8,128)(2,1)S(1)} %copy-done, bf16[64,512]{1,0:T(8,128)(2,1)} %param.13, bf16[512,512]{1,0:T(8,128)(2,1)} %param.11), kind=kOutput, calls=%fused_computation.2 | convolution fusion | flops 34603008 | bytes 1179648 | tf_op jit(solution)/shard_map/dot_general | solution.py:22
  10.2 0.0 all-gather.2.cloned.1.call-update
  10.2 0.7 add_convert_fusion
  10.9 0.6 stack.2
  11.5 8.3 %all-to-all-start = ((bf16[16,1,128]{2,1,0:T(2,128)(2,1)}), bf16[16,1,128]{2,1,0:T(2,128)(2,1)S(1)}, u32[]{:S(2)}, u32[]{:S(2)}) async-start(bf16[16,1,128]{2,1,0:T(2,128)(2,1)} %stack.2), calls=%async_computation | async-start | bytes 16384 | tf_op jit(solution)/shard_map/all_to_all | solution.py:45
  19.8 1.2 %fusion.4 = bf16[512,128]{1,0:T(8,128)(2,1)S(1)} fusion(bf16[512,64]{0,1:T(8,128)(2,1)} %param.15, bf16[64,128]{1,0:T(8,128)(2,1)} %param.16, bf16[512,128]{1,0:T(8,128)(2,1)} %param.14), kind=kOutput, calls=%fused_computation.7 | convolution fusion | flops 8650752 | bytes 344064 | tf_op jit(solution)/shard_map/dot_general | solution.py:25
  21.1 23.2 %all_gather.10 = bf16[2048,128]{1,0:T(8,128)(2,1)S(1)} all-gather(bf16[512,128]{1,0:T(8,128)(2,1)S(1)} %fusion.4), channel_id=1, replica_groups=mesh['rows'=4,'tp'=4,'unit'=2] {'rows'}, dimensions={0}, use_global_device_ids=true | all-gather | bytes 655360 | tf_op jit(solution)/shard_map/all_gather | solution.py:38
  44.2 0.0 copy-done.1
  44.2 0.0 copy-done.2
  44.2 0.0 copy-done.3
  44.2 0.2 fusion.5
  44.4 22.3 %all_gather.11 = bf16[2048,128]{1,0:T(8,128)(2,1)S(1)} all-gather(bf16[512,128]{1,0:T(8,128)(2,1)S(1)} %fusion.5), channel_id=1, replica_groups=mesh['rows'=4,'tp'=4,'unit'=2] {'rows'}, dimensions={0}, use_global_device_ids=true | all-gather | bytes 655360 | tf_op jit(solution)/shard_map/all_gather | solution.py:39
  66.8 1.0 %copy.22 = bf16[128,2048]{1,0:T(8,128)(2,1)} copy(bf16[128,2048]{0,1:T(8,128)(2,1)S(1)} %bitcast.10) | data formatting | bytes 1048576
  67.8 1.0 %copy.23 = bf16[128,2048]{1,0:T(8,128)(2,1)} copy(bf16[128,2048]{0,1:T(8,128)(2,1)S(1)} %bitcast.11) | data formatting | bytes 1048576
  68.8 0.0 all-to-all-done
  68.8 0.6 reduce
  69.4 6.3 %all-gather.2.cloned.1.call-done = bf16[2048,512]{1,0:T(8,128)(2,1)} async-done(((bf16[512,512]{1,0:T(8,128)(2,1)}), bf16[2048,512]{1,0:T(8,128)(2,1)}) %all-gather.2.cloned.1.call-update) | async-done | bytes 2097168 | tf_op jit(solution)/shard_map/all_gather | solution.py:37
  75.7 3.9 %copy.21 = bf16[512,2048]{1,0:T(8,128)(2,1)} copy(bf16[512,2048]{0,1:T(8,128)(2,1)} %bitcast.12) | data formatting | bytes 4194304
Async XLA Ops:
  7.2 0.8 copy-start
  7.2 37.0 %copy-start.1 = (bf16[512,128]{1,0:T(8,128)(2,1)S(1)}, bf16[512,128]{1,0:T(8,128)(2,1)}, u32[]{:S(2)}) copy-start(bf16[512,128]{1,0:T(8,128)(2,1)} %param.17) | copy-start | bytes 393220
  7.2 37.0 %copy-start.2 = (bf16[512,64]{0,1:T(8,128)(2,1)S(1)}, bf16[512,64]{0,1:T(8,128)(2,1)}, u32[]{:S(2)}) copy-start(bf16[512,64]{0,1:T(8,128)(2,1)} %param.18) | copy-start | bytes 196612
  7.2 37.0 %copy-start.3 = (bf16[64,128]{1,0:T(8,128)(2,1)S(1)}, bf16[64,128]{1,0:T(8,128)(2,1)}, u32[]{:S(2)}) copy-start(bf16[64,128]{1,0:T(8,128)(2,1)} %param.19) | copy-start | bytes 49156
  7.2 68.5 %all-gather.2.cloned.1.call-start = ((), (), s32[]{:S(2)}) async-start(), calls=%async_computation.1 | async-start | bytes 2621440 | tf_op jit(solution)/shard_map/all_gather | solution.py:37
  11.5 57.3 %all-to-all-start = ((bf16[16,1,128]{2,1,0:T(2,128)(2,1)}), bf16[16,1,128]{2,1,0:T(2,128)(2,1)S(1)}, u32[]{:S(2)}, u32[]{:S(2)}) async-start(bf16[16,1,128]{2,1,0:T(2,128)(2,1)} %stack.2), calls=%async_computation | async-start | bytes 16384 | tf_op jit(solution)/shard_map/all_to_all | solution.py:45
Sparse Core Ops, SparseCore 0:
  10.3 65.2 all-gather.1
